TPU v7x, 32 devices: a whole 2x2x4 slice. The times are simulated.
32 devices in a mesh: grp: 4 (over z), fsdp: 4 (over y, x), tp: 2 (over core).
Axes of the slice: x: 2, y: 2, z: 4, core: 2. Of those that a mesh axis runs over, the one named last changes fastest.
Arguments:
- frames: bfloat16 [768, 5120], P('fsdp', 'grp'), may hold values from -6 to 6
- projector: bfloat16 [5120, 8192], P('grp', 'tp'), may hold values from -0.078125 to 0.078125
- text_token_embedding: bfloat16 [4096, 8192], P(('grp', 'fsdp'), 'tp'), may hold values from -6 to 6
- norm_gain_vector: float32 [8192], replicated, may hold values from 0.1 to 1.9
- frozen: bfloat16 [8192, 1024], P('fsdp', 'tp'), may hold values from -0.0625 to 0.0625
- adapter_down_map: bfloat16 [8192, 64], P('fsdp'), may hold values from -0.0625 to 0.0625
- adapter_up_map: bfloat16 [64, 1024], P(None, 'tp'), may hold values from -0.75 to 0.75
- clip_frame_length: int32 [4, 4, 4], P('fsdp'), may hold values from 1 to 24, as said below
- audio_first_token: int32 [4, 4, 4], P('fsdp'), may hold values from 0 to 255, as said below
- segment_document_index: int32 [4096], P(('grp', 'fsdp')), may hold values from 0 to 63, never falling along the last dimension, each value on 1 to 256 neighbouring positions
- keep_document_flags: int32 [64], replicated, may hold values 0 or 1
- cotangent: bfloat16 [4096, 1024], P(('grp', 'fsdp'), 'tp'), may hold values from -0.09375 to 0.09375
Outputs:
- value_output: bfloat16 [4096, 1024], P(('grp', 'fsdp'), 'tp')
- projector_grad: float32 [5120, 8192], P('grp', 'tp')
- down_map_gradient: float32 [8192, 64], P('tp')
- up_map_gradient: float32 [64, 1024], P(None, 'tp')
Inputs may be any that keep to these rules, and one draw needn't show every extreme that they name: `clip_frame_length`: entry [f, g, k] is the length of clip k of frame block f * 4 + g; the 4 clips of a block sum to 48, and one of them has exactly 24 frames. `audio_first_token`: entry [f, g, k] is the first token, among the 256 tokens of block k * 4 + f, of the audio slots of clip k of frame block f * 4 + g; the 4 clips that one token block takes lie in distinct aligned windows of 64 tokens.
All inputs are finite; a program needn't handle non-finite values.
Results may differ from a plain program's by a relative error of at most 0.018.
Values may be sent and summed in bfloat16 or wider, within the bound.
A program may use at most 128 MiB of HBM per device.

v0:
```python
import jax
import jax.numpy as jnp
from jax import lax
from jax.sharding import PartitionSpec as P

adapter_scale = 2.0
norm_eps = 1e-05
plane = ("fsdp", "tp")


def contract_leading(left_side, right_side):
    return lax.dot_general(
        left_side, right_side, (((0,), (0,)), ((), ())), preferred_element_type=jnp.float32
    )


def contract_trailing(left_side, right_side):
    return lax.dot_general(
        left_side, right_side, (((1,), (1,)), ((), ())), preferred_element_type=jnp.float32
    )


def block_perm(f_size, t_size, shift):
    pairs = []
    for f_src in range(f_size):
        for t_src in range(t_size):
            b = f_src * t_size + (t_src + shift) % t_size
            pairs.append((f_src * t_size + t_src, b % f_size * t_size + b // f_size))
    return pairs


def shards(
    frames,
    projector,
    text_token_embedding,
    norm_gain_vector,
    frozen,
    adapter_down_map,
    adapter_up_map,
    clip_frame_length,
    audio_first_token,
    segment_document_index,
    keep_document_flags,
    cotangent,
):
    g_idx, f_idx, t_idx = (lax.axis_index("grp"), lax.axis_index("fsdp"), lax.axis_index("tp"))
    f_size, t_size = (lax.axis_size("fsdp"), lax.axis_size("tp"))
    tok, width = text_token_embedding.shape
    groups = clip_frame_length.shape[1]
    block_frames = frames.shape[0]
    per_group = block_frames // groups
    cols = width // f_size
    full_width = width * t_size
    v_shard = frozen.shape[1]
    v_full = v_shard * t_size
    rank = adapter_down_map.shape[1]
    frames_all = lax.all_gather(frames, "fsdp", axis=0, tiled=True)
    clips = lax.all_gather(jnp.stack([clip_frame_length[0], audio_first_token[0]]), "fsdp", axis=0)
    text = lax.all_to_all(
        text_token_embedding.reshape(tok, f_size, cols).transpose(1, 0, 2),
        "fsdp",
        split_axis=0,
        concat_axis=0,
        tiled=True,
    )
    own_block = t_idx * f_size + f_idx
    own_j = lax.rem(own_block, t_size)
    frozen_own = jnp.zeros((cols, v_full), jnp.bfloat16)
    for shift in range(t_size):
        j = lax.rem(t_idx + shift, t_size)
        piece = lax.ppermute(
            lax.dynamic_slice_in_dim(frozen, j * cols, cols, 0),
            plane,
            block_perm(f_size, t_size, shift),
        )
        t_src = lax.rem(own_j - shift + t_size, t_size)
        frozen_own = lax.dynamic_update_slice_in_dim(frozen_own, piece, t_src * v_shard, 1)
    down_own = lax.ppermute(
        lax.dynamic_slice_in_dim(adapter_down_map, t_idx * cols, cols, 0),
        plane,
        block_perm(f_size, t_size, 0),
    )
    gain_own = lax.dynamic_slice_in_dim(norm_gain_vector, t_idx * width + f_idx * cols, cols, 0)
    sizes, firsts = (clips[:, 0], clips[:, 1])
    ends = jnp.cumsum(sizes, axis=2)
    pick = lax.broadcasted_iota(jnp.int32, sizes.shape, 2) == g_idx
    size_in = jnp.sum(jnp.where(pick, sizes, 0), axis=2)
    start_in = jnp.sum(jnp.where(pick, ends - sizes, 0), axis=2)
    first_in = jnp.sum(jnp.where(pick, firsts, 0), axis=2)
    base_row = lax.broadcasted_iota(jnp.int32, size_in.shape, 1) * per_group + start_in
    token_iota = lax.broadcasted_iota(jnp.int32, (f_size, tok, groups), 1)
    offset = token_iota - first_in[:, None, :]
    live = (offset >= 0) & (offset < size_in[:, None, :])
    is_audio = jnp.any(live, axis=2)
    row = jnp.sum(jnp.where(live, base_row[:, None, :] + offset, 0), axis=2)
    row = jnp.where(is_audio, row, -1)
    frame_iota = lax.broadcasted_iota(jnp.int32, (f_size, tok, block_frames), 2)
    take = (row[:, :, None] == frame_iota).astype(jnp.bfloat16)
    take_own = lax.dynamic_index_in_dim(take, f_idx, 0, keepdims=False)
    doc_iota = lax.broadcasted_iota(jnp.int32, (tok, keep_document_flags.shape[0]), 1)
    weight_tok = jnp.sum(
        jnp.where(segment_document_index[:, None] == doc_iota, keep_document_flags[None, :], 0),
        axis=1,
    )
    grad_out = cotangent * weight_tok.astype(jnp.bfloat16)[:, None]
    both = lax.all_gather(
        jnp.concatenate([grad_out, adapter_up_map], axis=0), "tp", axis=1, tiled=True
    )
    grad_full, up_full = (both[:tok], both[tok:])
    lora_tok = (adapter_scale * contract_trailing(grad_full, up_full)).astype(jnp.bfloat16)
    lora_plane = lax.all_gather(lora_tok, "fsdp", axis=0, tiled=True)
    grad_rows = lax.psum(contract_leading(take_own, grad_full).astype(jnp.bfloat16), "grp")
    grad_rows = lax.all_gather(grad_rows, "fsdp", axis=0, tiled=True)
    lora_rows = (adapter_scale * contract_trailing(grad_rows, up_full)).astype(jnp.bfloat16)
    grad_norm = contract_trailing(grad_rows, frozen_own) + contract_trailing(lora_rows, down_own)
    projector_own = lax.dynamic_slice_in_dim(projector, f_idx * cols, cols, 1)
    embedded = lax.psum(
        jnp.dot(frames_all, projector_own, preferred_element_type=jnp.float32).astype(jnp.bfloat16),
        "grp",
    )
    audio = lax.dot_general(
        take,
        embedded.reshape(f_size, block_frames, cols),
        (((2,), (1,)), ((0,), (0,))),
        preferred_element_type=jnp.float32,
    ).astype(jnp.bfloat16)
    x = jnp.where(is_audio[:, :, None], audio, text).reshape(f_size * tok, cols)
    x32 = x.astype(jnp.float32)
    e32 = embedded.astype(jnp.float32)
    stats = lax.psum(
        jnp.concatenate(
            [
                jnp.sum(x32 * x32, axis=1),
                jnp.sum(e32 * e32, axis=1),
                jnp.sum(e32 * gain_own[None, :] * grad_norm, axis=1),
            ]
        ),
        plane,
    )
    n_tok, n_frames = (f_size * tok, f_size * block_frames)
    inv_tok = lax.rsqrt(stats[:n_tok] / full_width + norm_eps)
    inv_frame = lax.rsqrt(stats[n_tok : n_tok + n_frames] / full_width + norm_eps)
    dots = inv_frame * stats[n_tok + n_frames :]
    frame_grad = (
        inv_frame[:, None] * gain_own[None, :] * grad_norm
        - e32 * (inv_frame * inv_frame * dots / full_width)[:, None]
    ).astype(jnp.bfloat16)
    frame_grad = lax.all_gather(frame_grad, "fsdp", axis=1, tiled=True)
    projector_grad = contract_leading(frames_all, frame_grad)
    normed = (x32 * inv_tok[:, None] * gain_own[None, :]).astype(jnp.bfloat16)
    low_part = jnp.dot(normed, down_own, preferred_element_type=jnp.float32)
    value_part = jnp.dot(normed, frozen_own, preferred_element_type=jnp.float32)
    value_part = value_part + adapter_scale * jnp.dot(
        low_part.astype(jnp.bfloat16), up_full, preferred_element_type=jnp.float32
    )
    value_part = value_part.astype(jnp.bfloat16).reshape(f_size, tok, t_size, v_shard)
    low_send = jnp.broadcast_to(
        low_part.astype(jnp.bfloat16).reshape(f_size, tok, 1, rank), (f_size, tok, t_size, rank)
    )
    sent = (
        jnp.concatenate([value_part, low_send], axis=3)
        .transpose(0, 2, 1, 3)
        .reshape(f_size * t_size, tok, v_shard + rank)
    )
    got = lax.all_to_all(sent, plane, split_axis=0, concat_axis=0, tiled=True)
    total = jnp.sum(got.astype(jnp.float32), axis=0)
    value_output = total[:, :v_shard].astype(jnp.bfloat16)
    low_half = total[:, v_shard:].astype(jnp.bfloat16)
    up_part = adapter_scale * contract_leading(low_half, grad_out)
    down_part = contract_leading(normed, lora_plane)
    down_sum, up_sum = lax.psum((down_part, up_part), "grp")
    gathered = lax.all_gather(
        jnp.concatenate([down_sum, up_sum.reshape(-1, rank)], axis=0), "fsdp", axis=0
    )
    down_map_gradient = gathered[:, :cols].reshape(width, rank)
    up_map_gradient = jnp.sum(gathered[:, cols:], axis=0).reshape(rank, v_shard)
    return (value_output, projector_grad, down_map_gradient, up_map_gradient)


def solution(mesh):
    in_specs = (
        P("fsdp", "grp"),
        P("grp", "tp"),
        P(("grp", "fsdp"), "tp"),
        P(),
        P("fsdp", "tp"),
        P("fsdp", None),
        P(None, "tp"),
        P("fsdp", None, None),
        P("fsdp", None, None),
        P(("grp", "fsdp")),
        P(),
        P(("grp", "fsdp"), "tp"),
    )
    out_specs = (P(("grp", "fsdp"), "tp"), P("grp", "tp"), P("tp", None), P(None, "tp"))
    return jax.shard_map(shards, mesh=mesh, in_specs=in_specs, out_specs=out_specs, check_vma=False)
```

profile of v0, /device:TPU:0, one launch (start us, length us, event | category | flops | bytes accessed | tf_op | source)
XLA Modules:
  0.0 499.5 jit_solution(9193602135876863072)
XLA Ops:
  7.2 0.7 all-gather.7.cloned.1.call-update
  8.0 0.8 select_reduce_fusion
  8.8 0.7 pad_add_fusion
  9.5 9.7 %all-gather = s32[8,4,4]{2,1,0:T(4,128)S(1)} all-gather(s32[2,4,4]{2,1,0:T(4,128)S(1)} %pad_add_fusion), channel_id=2, replica_groups=mesh['grp'=4,'fsdp'=4,'tp'=2] {'fsdp'}, dimensions={0}, use_global_device_ids=true | all-gather | bytes 640 | tf_op jit(solution)/shard_map/all_gather | solution.py:58
  19.2 0.7 reduce_window_sum.11
  19.9 0.3 select_reduce_fusion.2
  20.2 0.1 fusion.42
  20.3 0.1 select_reduce_fusion.1
  20.4 1.1 broadcast_multiply_fusion
  21.5 0.9 pad_maximum_fusion.2
  22.4 2.3 all_gather.30
  24.6 0.1 iota_compare_fusion
  24.7 1.0 convolution_convert_fusion
  25.8 20.9 %all-gather.7.cloned.1.call-done = bf16[768,1280]{1,0:T(8,128)(2,1)} async-done(((bf16[192,1280]{1,0:T(8,128)(2,1)}), bf16[768,1280]{1,0:T(8,128)(2,1)}) %all-gather.7.cloned.1.call-update) | async-done | bytes 1966096 | tf_op jit(solution)/shard_map/all_gather | solution.py:57
  46.7 5.7 %fusion.12 = bf16[768,1024]{0,1:T(8,128)(2,1)} fusion(bf16[768,1280]{1,0:T(8,128)(2,1)} %all-gather.7.cloned.1.call-done, bf16[1280,4096]{1,0:T(8,128)(2,1)} %param.13, s32[]{:T(128)S(6)} %select_n.60), kind=kOutput, calls=%fused_computation.20 | convolution fusion | flops 2014052352 | bytes 6160388 | tf_op jit(solution)/shard_map/dot_general | solution.py:118
  52.5 82.0 %all-reduce.7.cloned.1.call-done = (bf16[768,1024]{0,1:T(8,128)(2,1)}, bf16[192,1024]{1,0:T(8,128)(2,1)}) async-done(((bf16[768,1024]{0,1:T(8,128)(2,1)}, bf16[192,1024]{1,0:T(8,128)(2,1)}), (bf16[768,1024]{0,1:T(8,128)(2,1)}, bf16[192,1024]{1,0:T(8,128)(2,1)})) %all-reduce.7.cloned.1.call-update) | async-done | bytes 1966096 | tf_op jit(solution)/shard_map/psum | solution.py:117
  134.5 3.3 copy.56
  137.8 2.4 copy.57
  140.2 3.6 all-to-all-start
  143.8 3.0 constant_dynamic-slice_fusion
  146.8 9.4 %collective-permute-start = (bf16[1024,512]{1,0:T(8,128)(2,1)}, bf16[1024,512]{1,0:T(8,128)(2,1)}, u32[]{:S(2)}, u32[]{:S(2)}) collective-permute-start(bf16[1024,512]{1,0:T(8,128)(2,1)} %get-tuple-element.30), channel_id=1, source_target_pairs={{0,0},{1,2},{2,4},{3,6},{4,1},{5,3},{6,5},{7,7},{8,8},{9,10},{10,1... | collective-permute-start | bytes 3145736 | tf_op jit(solution)/shard_map/ppermute | solution.py:71
  156.3 0.7 collective-permute-start.2
  157.0 0.7 dynamic_slice.20
  157.7 1.6 broadcast_in_dim.61
  159.3 2.3 constant_dynamic-update-slice_fusion.1
  161.6 40.1 %collective-permute-done.1 = bf16[1024,512]{1,0:T(8,128)(2,1)} collective-permute-done((bf16[1024,512]{1,0:T(8,128)(2,1)}, bf16[1024,512]{1,0:T(8,128)(2,1)}, u32[]{:S(2)}, u32[]{:S(2)}) %collective-permute-start.1) | collective-permute-done | bytes 1048608 | tf_op jit(solution)/shard_map/ppermute | solution.py:71
  201.7 2.3 constant_dynamic-update-slice_fusion
  204.0 2.6 copy.55
  206.6 4.5 multiply_reduce_fusion
  211.2 4.3 fusion.16
  215.5 6.7 %fusion.2 = (f32[768]{0:T(1024)S(1)}, f32[768]{0:T(1024)S(1)}, f32[768,1024]{0,1:T(8,128)}) fusion(bf16[768,1024]{0,1:T(8,128)(2,1)S(1)} %copy-done.2, f32[1024]{0:T(1024)S(1)} %dynamic_slice.20, f32[768,1024]{0,1:T(8,128)} %fusion.16, bf16[768,1024]{1,0:T(8,128)(2,1)} %all-gather.9.cloned.1.call-done, bf16[1024,1024]{1,0:T(8,128)(2,1)} %constant_dynamic-update-slice_fusion), kind=kOutput, calls=%fused_computation.9 | convolution fusion | flops 1616116224 | bytes 11544576 | tf_op jit(solution)/shard_map/dot_general | solution.py:18
  222.2 27.2 %psum.37 = f32[2560]{0:T(1024)S(1)} all-reduce(f32[2560]{0:T(1024)S(1)} %pad_maximum_fusion.3), channel_id=1, replica_groups=mesh['grp'=4,'fsdp'=4,'tp'=2] {'fsdp','tp'}, use_global_device_ids=true, to_apply=%region_12.13 | all-reduce | flops 2560 | bytes 20480 | tf_op jit(solution)/shard_map/psum | solution.py:130
  249.3 2.6 fusion.1
  252.0 0.8 convolution_convert_fusion.1
  252.7 0.7 fusion.23
  253.5 5.3 %add_convert_fusion = bf16[1024,1024]{1,0:T(8,128)(2,1)} fusion(f32[1024,1024]{1,0:T(8,128)S(1)} %fusion.23, bf16[1024,1024]{1,0:T(8,128)(2,1)S(1)} %fusion.1, bf16[1024,1024]{1,0:T(8,128)(2,1)} %constant_dynamic-update-slice_fusion), kind=kOutput, calls=%fused_computation.7 | convolution fusion | flops 2150629376 | bytes 10485760 | tf_op jit(solution)/shard_map/dot_general | solution.py:152
  258.7 4.5 reshape.66
  263.2 6.1 %copy.61 = bf16[4,256,2,512]{1,3,2,0:T(8,128)(2,1)} copy(bf16[4,256,2,512]{3,2,1,0:T(2,128)(2,1)} %reshape.66) | data formatting | bytes 4194304 | tf_op jit(solution)/shard_map/reshape | solution.py:156
  269.4 3.2 pad_maximum_fusion
  272.5 4.4 all-to-all-start.1
  276.9 0.0 all-reduce.5.cloned.1.call-start
  277.0 0.3 fusion.17
  277.2 32.5 %all_gather.33 = bf16[1024,64]{0,1:T(8,128)(2,1)S(1)} all-gather(bf16[256,64]{0,1:T(8,128)(2,1)S(1)} %fusion.17), channel_id=1, replica_groups=mesh['grp'=4,'fsdp'=4,'tp'=2] {'fsdp'}, dimensions={0}, use_global_device_ids=true | all-gather | bytes 163840 | tf_op jit(solution)/shard_map/all_gather | solution.py:111
  309.8 1.2 fusion.44
  311.0 2.2 reduce.1
  313.2 0.2 convolution_multiply_fusion.1
  313.4 0.1 reshape.68
  313.5 0.8 copy.62
  314.3 0.0 all-gather.13.cloned.1.call-start
  314.3 35.8 %all-reduce.5.cloned.1.call-done = (f32[512,64]{0,1:T(8,128)}, f32[1024,64]{0,1:T(8,128)}) async-done(((f32[512,64]{0,1:T(8,128)}, f32[1024,64]{0,1:T(8,128)}), (f32[512,64]{0,1:T(8,128)}, f32[1024,64]{0,1:T(8,128)})) %all-reduce.5.cloned.1.call-update) | async-done | bytes 393232 | tf_op jit(solution)/shard_map/psum | solution.py:171
  350.1 1.8 pad_maximum_fusion.1
  351.9 0.3 all-gather.11.cloned.1.call-start
  352.2 3.6 fusion.6
  355.9 0.8 copy.64
  356.7 26.3 %all-gather.13.cloned.1.call-done = f32[6144,64]{0,1:T(8,128)} async-done(((f32[1536,64]{0,1:T(8,128)}), f32[6144,64]{0,1:T(8,128)}) %all-gather.13.cloned.1.call-update) | async-done | bytes 1572880 | tf_op jit(solution)/shard_map/all_gather | solution.py:172
  383.0 2.4 reshape.73
  385.4 0.1 slice.55
  385.6 1.6 copy.70
  387.1 0.2 slice_reduce_fusion
  387.4 0.1 copy.63
  387.5 0.8 reshape.70
  388.3 67.0 %all-gather.11.cloned.1.call-done = bf16[768,4096]{0,1:T(8,128)(2,1)} async-done(((bf16[768,1024]{0,1:T(8,128)(2,1)}), bf16[768,4096]{0,1:T(8,128)(2,1)}) %all-gather.11.cloned.1.call-update) | async-done | bytes 6291472 | tf_op jit(solution)/shard_map/all_gather | solution.py:148
  455.3 14.9 %convolution_bitcast_fusion = f32[1280,4096]{0,1:T(8,128)} fusion(bf16[768,4096]{0,1:T(8,128)(2,1)} %all-gather.11.cloned.1.call-done, bf16[768,1280]{1,0:T(8,128)(2,1)} %all-gather.7.cloned.1.call-done), kind=kOutput, calls=%fused_computation | convolution fusion | flops 8053063680 | bytes 29229056 | tf_op jit(solution)/shard_map/dot_general | solution.py:12
  470.2 22.4 %copy.65 = f32[1280,4096]{1,0:T(8,128)} copy(f32[1280,4096]{0,1:T(8,128)} %convolution_bitcast_fusion) | data formatting | bytes 41943040
  (38 shorter events, 0.4 us)
Async XLA Ops:
  7.2 149.1 %copy-start = (bf16[2048,64]{0,1:T(8,128)(2,1)S(1)}, bf16[2048,64]{0,1:T(8,128)(2,1)}, u32[]{:S(2)}) copy-start(bf16[2048,64]{0,1:T(8,128)(2,1)} %param.17) | copy-start | bytes 786436
  7.2 39.5 %all-gather.7.cloned.1.call-start = ((), (), s32[]{:S(2)}) async-start(), calls=%async_computation.2 | async-start | bytes 2457600 | tf_op jit(solution)/shard_map/all_gather | solution.py:57
  7.9 126.6 %all-reduce.7.cloned.1.call-start = ((), (), s32[]{:S(2)}) async-start(), calls=%async_computation.7 | async-start | bytes 3932160 | tf_op jit(solution)/shard_map/psum | solution.py:117
  52.5 158.7 %all-gather.9.cloned.1.call-start = ((), (), s32[]{:S(2)}) async-start(), calls=%async_computation.3 | async-start | bytes 1966080 | tf_op jit(solution)/shard_map/all_gather | solution.py:113
  140.2 66.4 %all-to-all-start = ((bf16[4,256,1024]{2,1,0:T(8,128)(2,1)}), bf16[4,256,1024]{2,1,0:T(8,128)(2,1)S(1)}, u32[]{:S(2)}, u32[]{:S(2)}) async-start(bf16[4,256,1024]{2,1,0:T(8,128)(2,1)} %bitcast.60), calls=%async_computation | async-start | bytes 4194304 | tf_op jit(solution)/shard_map/all_to_all | solution.py:59
  146.8 10.9 %collective-permute-start = (bf16[1024,512]{1,0:T(8,128)(2,1)}, bf16[1024,512]{1,0:T(8,128)(2,1)}, u32[]{:S(2)}, u32[]{:S(2)}) collective-permute-start(bf16[1024,512]{1,0:T(8,128)(2,1)} %get-tuple-element.30), channel_id=1, source_target_pairs={{0,0},{1,2},{2,4},{3,6},{4,1},{5,3},{6,5},{7,7},{8,8},{9,10},{10,1... | collective-permute-start | bytes 3145736 | tf_op jit(solution)/shard_map/ppermute | solution.py:71
  156.3 45.4 %collective-permute-start.1 = (bf16[1024,512]{1,0:T(8,128)(2,1)}, bf16[1024,512]{1,0:T(8,128)(2,1)}, u32[]{:S(2)}, u32[]{:S(2)}) collective-permute-start(bf16[1024,512]{1,0:T(8,128)(2,1)} %get-tuple-element.29), channel_id=1, source_target_pairs={{0,2},{1,0},{2,6},{3,4},{4,3},{5,1},{6,7},{7,5},{8,10},{9,8},{10,1... | collective-permute-start | bytes 3145736 | tf_op jit(solution)/shard_map/ppermute | solution.py:71
  156.3 54.8 %collective-permute-start.2 = (bf16[1024,64]{0,1:T(8,128)(2,1)S(1)}, bf16[1024,64]{0,1:T(8,128)(2,1)S(1)}, u32[]{:S(2)}, u32[]{:S(2)}) collective-permute-start(bf16[1024,64]{0,1:T(8,128)(2,1)S(1)} %constant_dynamic-slice_fusion.2), channel_id=1, source_target_pairs={{0,0},{1,2},{2,4},{3,6},{4,1},{5,3},{6,5},{7,7},{8,8},{9,10},{10,1... | collective-permute-start | bytes 393224 | tf_op jit(solution)/shard_map/ppermute | solution.py:78
  211.1 4.3 copy-start.2
  272.5 38.4 %all-to-all-start.1 = ((bf16[8,256,576]{1,2,0:T(8,128)(2,1)}), bf16[8,256,576]{1,2,0:T(8,128)(2,1)}, u32[]{:S(2)}, u32[]{:S(2)}) async-start(bf16[8,256,576]{1,2,0:T(8,128)(2,1)} %bitcast.59), calls=%async_computation.1 | async-start | bytes 4718592 | tf_op jit(solution)/shard_map/all_to_all | solution.py:165
  276.9 73.2 %all-reduce.5.cloned.1.call-start = ((), (), s32[]{:S(2)}) async-start(), calls=%async_computation.6 | async-start | bytes 786432 | tf_op jit(solution)/shard_map/psum | solution.py:171
  310.9 41.2 %copy-start.3 = (bf16[768,1024]{0,1:T(8,128)(2,1)S(1)}, bf16[768,1024]{0,1:T(8,128)(2,1)}, u32[]{:S(2)}) copy-start(bf16[768,1024]{0,1:T(8,128)(2,1)} %get-tuple-element.27) | copy-start | bytes 4718596
  314.3 68.8 %all-gather.13.cloned.1.call-start = ((), (), s32[]{:S(2)}) async-start(), calls=%async_computation.5 | async-start | bytes 1966080 | tf_op jit(solution)/shard_map/all_gather | solution.py:172
  351.9 103.4 %all-gather.11.cloned.1.call-start = ((), (), s32[]{:S(2)}) async-start(), calls=%async_computation.4 | async-start | bytes 7864320 | tf_op jit(solution)/shard_map/all_gather | solution.py:148
  470.2 22.4 %copy-start.1 = (bf16[2048,64]{0,1:T(8,128)(2,1)S(1)}, bf16[2048,64]{0,1:T(8,128)(2,1)}, u32[]{:S(2)}) copy-start(bf16[2048,64]{0,1:T(8,128)(2,1)} %param.17) | copy-start | bytes 786436
Sparse Core Ops, SparseCore 0:
  9.8 36.8 all-gather.6
  52.6 81.8 all-reduce.6
  136.3 52.9 all-gather.8
  314.4 35.6 all-reduce.4
  352.3 30.6 all-gather.12
  385.3 70.0 all-gather.10
where the time goes:
time: 502 us; the launch traced here: 499 us
  waiting for transfers between devices  273 us (54%)
  blocking collectives  71.6 us (14%)
  local copies, waits for them, and re-layouts  58.1 us (12%)
  matrix products  45.5 us (9%)
  starting transfers between devices  18.6 us (4%)
  other arithmetic  18.5 us (4%)
  between operations  14.3 us (3%)
    psum x1, waiting for transfers between devices, shards(): lax.psum(jnp.dot(frames_all, projector_own, preferred_element_type=jnp.fl...  82 us
    all_gather x1, waiting for transfers between devices, shards(): frame_grad = lax.all_gather(frame_grad, 'fsdp', axis=1, tiled=True)  67 us
    ppermute x2, waiting for transfers between devices, shards(): lax.ppermute(lax.dynamic_slice_in_dim(frozen, j * cols, cols, 0), plane,...  40.1 us
    psum x1, waiting for transfers between devices, shards(): down_sum, up_sum = lax.psum((down_part, up_part), 'grp')  35.8 us
    all_gather x1, blocking collectives, shards(): lora_plane = lax.all_gather(lora_tok, 'fsdp', axis=0, tiled=True)  32.5 us
    unnamed x13, local copies, waits for them, and re-layouts  28.2 us
    psum x1, blocking collectives, shards(): lax.psum(jnp.concatenate([jnp.sum(x32 * x32, axis=1), jnp.sum(e32 * e32,...  27.2 us
    all_gather x1, waiting for transfers between devices, shards(): lax.all_gather(jnp.concatenate([down_sum, up_sum.reshape(-1, rank)], axis...  26.3 us
  transfers between devices with their start and end apart: 11, of which 6 were waited for; matrix products, arithmetic and copies ran while one was open for 8% of the time, Pallas kernels for 0%

commit v1 on v0

--- a/solution.py
+++ b/solution.py
@@ -145,7 +145,9 @@
         inv_frame[:, None] * gain_own[None, :] * grad_norm
         - e32 * (inv_frame * inv_frame * dots / full_width)[:, None]
     ).astype(jnp.bfloat16)
-    frame_grad = lax.all_gather(frame_grad, "fsdp", axis=1, tiled=True)
+    frame_grad = jnp.concatenate(
+        lax.all_to_all(jnp.stack([frame_grad] * lax.axis_size("fsdp")), "fsdp", 0, 0), axis=1
+    )
     projector_grad = contract_leading(frames_all, frame_grad)
     normed = (x32 * inv_tok[:, None] * gain_own[None, :]).astype(jnp.bfloat16)
     low_part = jnp.dot(normed, down_own, preferred_element_type=jnp.float32)

time: 502 us -> 484 us (0.964)
  waiting for transfers between devices: 273 us -> 206 us
  blocking collectives: 71.6 us -> 111 us
    all_gather x1 -> x0, waiting for transfers between devices: 67 us -> none  [shards(): frame_grad = lax.all_gather(frame_grad, 'fsdp', axis=1, tiled=True)]
    all_gather x1, blocking collectives: 32.5 us -> 72 us  [shards(): lora_plane = lax.all_gather(lora_tok, 'fsdp', axis=0, tiled=True)]
    all_gather x1, waiting for transfers between devices: 26.3 us -> 0.01 us  [shards(): lax.all_gather(jnp.concatenate([down_sum, up_sum.reshape(-1, rank)], axis...]
    all_to_all x1, waiting for transfers between devices: 0.01 us -> 25.3 us  [shards(): got = lax.all_to_all(sent, plane, split_axis=0, concat_axis=0, tiled=True)]
    all_to_all x0 -> x1, starting transfers between devices: none -> 5.26 us  [shards(): lax.all_to_all(jnp.stack([frame_grad] * lax.axis_size('fsdp')), 'fsdp', 0...]
  transfers between devices with their start and end apart: 11 -> 11, of which waited for: 6 -> 5; matrix products, arithmetic and copies ran while one was open for 8% -> 16% of each run, Pallas kernels for 0% -> 0%
where the time goes in v1:
time: 484 us; the launch traced here: 482 us
  waiting for transfers between devices  206 us (43%)
  blocking collectives  111 us (23%)
  local copies, waits for them, and re-layouts  62.6 us (13%)
  matrix products  45.3 us (9%)
  starting transfers between devices  23.6 us (5%)
  other arithmetic  18.8 us (4%)
  between operations  14 us (3%)
    psum x1, waiting for transfers between devices, shards(): lax.psum(jnp.dot(frames_all, projector_own, preferred_element_type=jnp.fl...  82 us
    all_gather x1, blocking collectives, shards(): lora_plane = lax.all_gather(lora_tok, 'fsdp', axis=0, tiled=True)  72 us
    ppermute x2, waiting for transfers between devices, shards(): lax.ppermute(lax.dynamic_slice_in_dim(frozen, j * cols, cols, 0), plane,...  40.1 us
    psum x1, waiting for transfers between devices, shards(): down_sum, up_sum = lax.psum((down_part, up_part), 'grp')  37.2 us
    unnamed x13, local copies, waits for them, and re-layouts  28.1 us
    psum x1, blocking collectives, shards(): lax.psum(jnp.concatenate([jnp.sum(x32 * x32, axis=1), jnp.sum(e32 * e32,...  27.2 us
    all_to_all x1, waiting for transfers between devices, shards(): got = lax.all_to_all(sent, plane, split_axis=0, concat_axis=0, tiled=True)  25.3 us
    all_gather x1, waiting for transfers between devices, shards(): frames_all = lax.all_gather(frames, 'fsdp', axis=0, tiled=True)  20.9 us
  transfers between devices with their start and end apart: 11, of which 5 were waited for; matrix products, arithmetic and copies ran while one was open for 16% of the time, Pallas kernels for 0%

profile of v1, /device:TPU:0, one launch (start us, length us, event | category | flops | bytes accessed | tf_op | source)
XLA Modules:
  0.0 481.6 jit_solution(986597594225435443)
XLA Ops:
  7.2 0.7 all-gather.6.cloned.1.call-update
  8.0 0.8 select_reduce_fusion
  8.8 0.7 pad_add_fusion
  9.5 9.7 %all-gather = s32[8,4,4]{2,1,0:T(4,128)S(1)} all-gather(s32[2,4,4]{2,1,0:T(4,128)S(1)} %pad_add_fusion), channel_id=2, replica_groups=mesh['grp'=4,'fsdp'=4,'tp'=2] {'fsdp'}, dimensions={0}, use_global_device_ids=true | all-gather | bytes 640 | tf_op jit(solution)/shard_map/all_gather | solution.py:58
  19.2 0.7 reduce_window_sum.11
  19.9 0.3 select_reduce_fusion.2
  20.2 0.1 fusion.42
  20.3 0.1 select_reduce_fusion.1
  20.4 1.1 broadcast_multiply_fusion
  21.5 0.9 pad_maximum_fusion.2
  22.4 2.3 all_gather.27
  24.6 0.1 iota_compare_fusion
  24.7 1.0 convolution_convert_fusion
  25.8 20.9 %all-gather.6.cloned.1.call-done = bf16[768,1280]{1,0:T(8,128)(2,1)} async-done(((bf16[192,1280]{1,0:T(8,128)(2,1)}), bf16[768,1280]{1,0:T(8,128)(2,1)}) %all-gather.6.cloned.1.call-update) | async-done | bytes 1966096 | tf_op jit(solution)/shard_map/all_gather | solution.py:57
  46.7 5.7 %fusion.12 = bf16[768,1024]{0,1:T(8,128)(2,1)} fusion(bf16[768,1280]{1,0:T(8,128)(2,1)} %all-gather.6.cloned.1.call-done, bf16[1280,4096]{1,0:T(8,128)(2,1)} %param.13, s32[]{:T(128)S(6)} %select_n.60), kind=kOutput, calls=%fused_computation.20 | convolution fusion | flops 2014052352 | bytes 6160388 | tf_op jit(solution)/shard_map/dot_general | solution.py:118
  52.5 82.0 %all-reduce.7.cloned.1.call-done = (bf16[768,1024]{0,1:T(8,128)(2,1)}, bf16[192,1024]{1,0:T(8,128)(2,1)}) async-done(((bf16[768,1024]{0,1:T(8,128)(2,1)}, bf16[192,1024]{1,0:T(8,128)(2,1)}), (bf16[768,1024]{0,1:T(8,128)(2,1)}, bf16[192,1024]{1,0:T(8,128)(2,1)})) %all-reduce.7.cloned.1.call-update) | async-done | bytes 1966096 | tf_op jit(solution)/shard_map/psum | solution.py:117
  134.5 3.3 copy.57
  137.8 2.4 copy.58
  140.2 3.6 all-to-all-start
  143.8 3.0 constant_dynamic-slice_fusion
  146.8 9.4 %collective-permute-start = (bf16[1024,512]{1,0:T(8,128)(2,1)}, bf16[1024,512]{1,0:T(8,128)(2,1)}, u32[]{:S(2)}, u32[]{:S(2)}) collective-permute-start(bf16[1024,512]{1,0:T(8,128)(2,1)} %get-tuple-element.30), channel_id=1, source_target_pairs={{0,0},{1,2},{2,4},{3,6},{4,1},{5,3},{6,5},{7,7},{8,8},{9,10},{10,1... | collective-permute-start | bytes 3145736 | tf_op jit(solution)/shard_map/ppermute | solution.py:71
  156.3 0.7 collective-permute-start.2
  157.0 0.7 dynamic_slice.20
  157.7 1.6 broadcast_in_dim.61
  159.3 2.3 constant_dynamic-update-slice_fusion.1
  161.6 40.1 %collective-permute-done.1 = bf16[1024,512]{1,0:T(8,128)(2,1)} collective-permute-done((bf16[1024,512]{1,0:T(8,128)(2,1)}, bf16[1024,512]{1,0:T(8,128)(2,1)}, u32[]{:S(2)}, u32[]{:S(2)}) %collective-permute-start.1) | collective-permute-done | bytes 1048608 | tf_op jit(solution)/shard_map/ppermute | solution.py:71
  201.7 2.3 constant_dynamic-update-slice_fusion
  204.0 2.6 copy.56
  206.6 4.5 multiply_reduce_fusion
  211.2 4.3 fusion.16
  215.5 6.7 %fusion.2 = (f32[768]{0:T(1024)S(1)}, f32[768]{0:T(1024)S(1)}, f32[768,1024]{0,1:T(8,128)}) fusion(bf16[768,1024]{0,1:T(8,128)(2,1)S(1)} %copy-done.2, f32[1024]{0:T(1024)S(1)} %dynamic_slice.20, f32[768,1024]{0,1:T(8,128)} %fusion.16, bf16[768,1024]{1,0:T(8,128)(2,1)} %all-gather.8.cloned.1.call-done, bf16[1024,1024]{1,0:T(8,128)(2,1)} %constant_dynamic-update-slice_fusion), kind=kOutput, calls=%fused_computation.9 | convolution fusion | flops 1616116224 | bytes 11544576 | tf_op jit(solution)/shard_map/dot_general | solution.py:18
  222.2 27.2 %psum.37 = f32[2560]{0:T(1024)S(1)} all-reduce(f32[2560]{0:T(1024)S(1)} %pad_maximum_fusion.3), channel_id=1, replica_groups=mesh['grp'=4,'fsdp'=4,'tp'=2] {'fsdp','tp'}, use_global_device_ids=true, to_apply=%region_12.13 | all-reduce | flops 2560 | bytes 20480 | tf_op jit(solution)/shard_map/psum | solution.py:130
  249.3 2.6 fusion.1
  252.0 0.8 convolution_convert_fusion.1
  252.7 0.7 fusion.23
  253.5 5.3 %add_convert_fusion = bf16[1024,1024]{1,0:T(8,128)(2,1)} fusion(f32[1024,1024]{1,0:T(8,128)S(1)} %fusion.23, bf16[1024,1024]{1,0:T(8,128)(2,1)S(1)} %fusion.1, bf16[1024,1024]{1,0:T(8,128)(2,1)} %constant_dynamic-update-slice_fusion), kind=kOutput, calls=%fused_computation.7 | convolution fusion | flops 2150629376 | bytes 10485760 | tf_op jit(solution)/shard_map/dot_general | solution.py:154
  258.7 4.5 reshape.74
  263.2 6.1 %copy.62 = bf16[4,256,2,512]{1,3,2,0:T(8,128)(2,1)} copy(bf16[4,256,2,512]{3,2,1,0:T(2,128)(2,1)} %reshape.74) | data formatting | bytes 4194304 | tf_op jit(solution)/shard_map/reshape | solution.py:158
  269.4 3.2 pad_maximum_fusion
  272.5 4.4 all-to-all-start.1
  276.9 4.1 fusion.6
  281.1 25.3 %all-to-all-done.1 = bf16[8,256,576]{1,2,0:T(8,128)(2,1)} async-done(((bf16[8,256,576]{1,2,0:T(8,128)(2,1)}), bf16[8,256,576]{1,2,0:T(8,128)(2,1)}, u32[]{:S(2)}, u32[]{:S(2)}) %all-to-all-start.1) | async-done | bytes 2359328 | tf_op jit(solution)/shard_map/all_to_all | solution.py:167
  306.3 4.5 stack.5
  310.9 5.3 %all-to-all-start.2 = ((bf16[4,768,1024]{1,2,0:T(8,128)(2,1)}), bf16[4,768,1024]{1,2,0:T(8,128)(2,1)}, u32[]{:S(2)}, u32[]{:S(2)}) async-start(bf16[4,768,1024]{1,2,0:T(8,128)(2,1)} %stack.5), calls=%async_computation.2 | async-start | bytes 12582912 | tf_op jit(solution)/shard_map/all_to_all | solution.py:149
  316.1 0.0 all-reduce.5.cloned.1.call-start
  316.2 0.3 fusion.17
  316.5 72.0 %all_gather.29 = bf16[1024,64]{0,1:T(8,128)(2,1)S(1)} all-gather(bf16[256,64]{0,1:T(8,128)(2,1)S(1)} %fusion.17), channel_id=1, replica_groups=mesh['grp'=4,'fsdp'=4,'tp'=2] {'fsdp'}, dimensions={0}, use_global_device_ids=true | all-gather | bytes 163840 | tf_op jit(solution)/shard_map/all_gather | solution.py:111
  388.5 1.2 fusion.44
  389.7 2.1 reduce.1
  391.8 0.2 convolution_multiply_fusion.1
  392.0 0.1 reshape.78
  392.1 0.8 copy.63
  392.9 0.0 all-gather.10.cloned.1.call-start
  392.9 37.2 %all-reduce.5.cloned.1.call-done = (f32[512,64]{0,1:T(8,128)}, f32[1024,64]{0,1:T(8,128)}) async-done(((f32[512,64]{0,1:T(8,128)}, f32[1024,64]{0,1:T(8,128)}), (f32[512,64]{0,1:T(8,128)}, f32[1024,64]{0,1:T(8,128)})) %all-reduce.5.cloned.1.call-update) | async-done | bytes 393232 | tf_op jit(solution)/shard_map/psum | solution.py:173
  430.1 1.8 pad_maximum_fusion.1
  431.9 0.8 copy.65
  432.8 14.6 %convolution_bitcast_fusion = f32[1280,4096]{0,1:T(8,128)} fusion(bf16[768,4096]{0,1:T(8,128)(2,1)} %bitcast.12, bf16[768,1280]{1,0:T(8,128)(2,1)S(1)} %copy-done.3), kind=kOutput, calls=%fused_computation | convolution fusion | flops 8053063680 | bytes 29229056 | tf_op jit(solution)/shard_map/dot_general | solution.py:12
  447.4 22.4 %copy.66 = f32[1280,4096]{1,0:T(8,128)} copy(f32[1280,4096]{0,1:T(8,128)} %convolution_bitcast_fusion) | data formatting | bytes 41943040
  469.8 2.4 reshape.83
  472.2 0.2 slice_reduce_fusion
  472.4 0.1 slice.55
  472.6 1.6 copy.71
  474.2 0.1 copy.64
  474.3 0.8 reshape.80
  (38 shorter events, 0.4 us)
Async XLA Ops:
  7.2 149.1 %copy-start = (bf16[2048,64]{0,1:T(8,128)(2,1)S(1)}, bf16[2048,64]{0,1:T(8,128)(2,1)}, u32[]{:S(2)}) copy-start(bf16[2048,64]{0,1:T(8,128)(2,1)} %param.17) | copy-start | bytes 786436
  7.2 39.5 %all-gather.6.cloned.1.call-start = ((), (), s32[]{:S(2)}) async-start(), calls=%async_computation.3 | async-start | bytes 2457600 | tf_op jit(solution)/shard_map/all_gather | solution.py:57
  7.9 126.6 %all-reduce.7.cloned.1.call-start = ((), (), s32[]{:S(2)}) async-start(), calls=%async_computation.7 | async-start | bytes 3932160 | tf_op jit(solution)/shard_map/psum | solution.py:117
  52.5 158.7 %all-gather.8.cloned.1.call-start = ((), (), s32[]{:S(2)}) async-start(), calls=%async_computation.4 | async-start | bytes 1966080 | tf_op jit(solution)/shard_map/all_gather | solution.py:113
  140.2 66.4 %all-to-all-start = ((bf16[4,256,1024]{2,1,0:T(8,128)(2,1)}), bf16[4,256,1024]{2,1,0:T(8,128)(2,1)S(1)}, u32[]{:S(2)}, u32[]{:S(2)}) async-start(bf16[4,256,1024]{2,1,0:T(8,128)(2,1)} %bitcast.63), calls=%async_computation | async-start | bytes 4194304 | tf_op jit(solution)/shard_map/all_to_all | solution.py:59
  146.8 10.9 %collective-permute-start = (bf16[1024,512]{1,0:T(8,128)(2,1)}, bf16[1024,512]{1,0:T(8,128)(2,1)}, u32[]{:S(2)}, u32[]{:S(2)}) collective-permute-start(bf16[1024,512]{1,0:T(8,128)(2,1)} %get-tuple-element.30), channel_id=1, source_target_pairs={{0,0},{1,2},{2,4},{3,6},{4,1},{5,3},{6,5},{7,7},{8,8},{9,10},{10,1... | collective-permute-start | bytes 3145736 | tf_op jit(solution)/shard_map/ppermute | solution.py:71
  156.3 45.4 %collective-permute-start.1 = (bf16[1024,512]{1,0:T(8,128)(2,1)}, bf16[1024,512]{1,0:T(8,128)(2,1)}, u32[]{:S(2)}, u32[]{:S(2)}) collective-permute-start(bf16[1024,512]{1,0:T(8,128)(2,1)} %get-tuple-element.29), channel_id=1, source_target_pairs={{0,2},{1,0},{2,6},{3,4},{4,3},{5,1},{6,7},{7,5},{8,10},{9,8},{10,1... | collective-permute-start | bytes 3145736 | tf_op jit(solution)/shard_map/ppermute | solution.py:71
  156.3 54.8 %collective-permute-start.2 = (bf16[1024,64]{0,1:T(8,128)(2,1)S(1)}, bf16[1024,64]{0,1:T(8,128)(2,1)S(1)}, u32[]{:S(2)}, u32[]{:S(2)}) collective-permute-start(bf16[1024,64]{0,1:T(8,128)(2,1)S(1)} %constant_dynamic-slice_fusion.2), channel_id=1, source_target_pairs={{0,0},{1,2},{2,4},{3,6},{4,1},{5,3},{6,5},{7,7},{8,8},{9,10},{10,1... | collective-permute-start | bytes 393224 | tf_op jit(solution)/shard_map/ppermute | solution.py:78
  211.1 4.3 copy-start.2
  272.5 33.8 %all-to-all-start.1 = ((bf16[8,256,576]{1,2,0:T(8,128)(2,1)}), bf16[8,256,576]{1,2,0:T(8,128)(2,1)}, u32[]{:S(2)}, u32[]{:S(2)}) async-start(bf16[8,256,576]{1,2,0:T(8,128)(2,1)} %bitcast.62), calls=%async_computation.1 | async-start | bytes 4718592 | tf_op jit(solution)/shard_map/all_to_all | solution.py:167
  310.9 121.9 %all-to-all-start.2 = ((bf16[4,768,1024]{1,2,0:T(8,128)(2,1)}), bf16[4,768,1024]{1,2,0:T(8,128)(2,1)}, u32[]{:S(2)}, u32[]{:S(2)}) async-start(bf16[4,768,1024]{1,2,0:T(8,128)(2,1)} %stack.5), calls=%async_computation.2 | async-start | bytes 12582912 | tf_op jit(solution)/shard_map/all_to_all | solution.py:149
  316.1 113.9 %all-reduce.5.cloned.1.call-start = ((), (), s32[]{:S(2)}) async-start(), calls=%async_computation.6 | async-start | bytes 786432 | tf_op jit(solution)/shard_map/psum | solution.py:173
  391.8 41.0 %copy-start.3 = (bf16[768,1280]{1,0:T(8,128)(2,1)S(1)}, bf16[768,1280]{1,0:T(8,128)(2,1)}, u32[]{:S(2)}) copy-start(bf16[768,1280]{1,0:T(8,128)(2,1)} %all-gather.6.cloned.1.call-done) | copy-start | bytes 5898244
  392.9 76.9 %all-gather.10.cloned.1.call-start = ((), (), s32[]{:S(2)}) async-start(), calls=%async_computation.5 | async-start | bytes 1966080 | tf_op jit(solution)/shard_map/all_gather | solution.py:174
  472.2 2.9 copy-start.1
Sparse Core Ops, SparseCore 0:
  9.8 36.8 all-gather.5
  52.6 81.8 all-reduce.6
  136.3 52.9 all-gather.7
  393.0 37.0 all-reduce.4
  432.3 30.4 all-gather.9
